TPU v7x, 32 devices: a whole 2x2x4 slice. The times are simulated.
32 devices in a mesh: gx: 8 (over z, x), gy: 4 (over y, core).
Axes of the slice: x: 2, y: 2, z: 4, core: 2. Of those that a mesh axis runs over, the one named last changes fastest.
Arguments:
- right_side: float32 [3, 224, 12432], P(None, 'gx', 'gy'), may hold values from -6 to 6
- guess: float32 [3, 224, 12432], P(None, 'gx', 'gy'), may hold values from -6 to 6
- material: int32 [32, 16, 16], P('gx', 'gy'), may hold values from 0 to 7
- lame: float32 [2, 8], replicated, may hold values from 0.5 to 2
- upper: float32 [1], replicated, may hold values from 3 to 6
- lower_ratio: float32 [1], replicated, may hold values from 0.05 to 0.3
Outputs:
- smoothed: float32 [3, 224, 12432], P(None, 'gx', 'gy')
- residual: float32 [3, 224, 12432], P(None, 'gx', 'gy')
All inputs are finite; a program needn't handle non-finite values.
Results may differ from a plain program's by a relative error of at most 0.0003.
Values sent between devices are 32-bit elements; how exact they have to be, the bound alone decides.
A program may use at most 128 MiB of HBM per device.

v0:
```python
import jax
import jax.numpy as jnp
import numpy as np
from jax import lax
from jax.sharding import PartitionSpec as P

DEG = 7
SWEEPS = 2
CHEB = 3


highest = lax.Precision.HIGHEST


def from_behind(value, axis, by):
    size = lax.axis_size(axis)
    return lax.ppermute(value, axis, [(i, (i + by) % size) for i in range(size)])


def legendre_pair(points, degree):
    prev_poly = points * 0.0 + 1.0
    this_poly = points * 1.0
    for order in range(2, degree + 1):
        next_poly = ((2 * order - 1) * points * this_poly - (order - 1) * prev_poly) / order
        prev_poly = this_poly
        this_poly = next_poly
    return (this_poly, prev_poly)


def gll_tables(degree):
    count = degree + 1
    points = -np.cos(np.pi * np.arange(count) / degree)
    for newton_step in range(60):
        this_poly, prev_poly = legendre_pair(points, degree)
        points = points - (points * this_poly - prev_poly) / (count * this_poly)
    values, unused_poly = legendre_pair(points, degree)
    weights = 2.0 / (degree * (degree + 1) * values**2)
    identity_np = np.eye(count)
    spacing = points[:, None] - points[None, :] + identity_np
    derivative = values[:, None] / (values[None, :] * spacing) * (1.0 - identity_np)
    derivative[0, 0] = -degree * (degree + 1) / 4.0
    derivative[degree, degree] = degree * (degree + 1) / 4.0
    stiff_ratio = (weights[:, None] * derivative**2).sum(0) / weights
    return (weights, derivative, stiff_ratio)


def clamped_gather(blocks):
    free_nodes = DEG * blocks - 1
    selector = np.zeros((free_nodes, blocks * (DEG + 1)), np.float32)
    for element in range(blocks):
        for node_idx in range(DEG + 1):
            target = DEG * element + node_idx - 1
            if 0 <= target < free_nodes:
                selector[target, element * (DEG + 1) + node_idx] = 1.0
    return selector


def split_open(field_in, dim_index):
    layout = field_in.shape
    blocks = (layout[dim_index] - 1) // DEG
    leading = lax.slice_in_dim(field_in, 0, blocks * DEG, axis=dim_index)
    leading = leading.reshape(layout[:dim_index] + (blocks, DEG) + layout[dim_index + 1 :])
    trailing = lax.slice_in_dim(field_in, DEG, blocks * DEG + 1, stride=DEG, axis=dim_index)
    trailing = jnp.expand_dims(trailing, dim_index + 1)
    return jnp.concatenate([leading, trailing], axis=dim_index + 1)


def fold_open(element_vals, dim_index):
    layout = element_vals.shape
    blocks = layout[dim_index]
    merged = layout[:dim_index] + (blocks * DEG,) + layout[dim_index + 2 :]
    leading = lax.slice_in_dim(element_vals, 0, DEG, axis=dim_index + 1).reshape(merged)
    trailing = lax.slice_in_dim(element_vals, DEG, DEG + 1, axis=dim_index + 1)
    widths = [(0, 0)] * len(layout)
    widths[dim_index + 1] = (DEG - 1, 0)
    spread_tail = jnp.pad(trailing, widths).reshape(merged)
    after_pad = [(0, 0)] * len(merged)
    after_pad[dim_index] = (0, 1)
    before_pad = [(0, 0)] * len(merged)
    before_pad[dim_index] = (1, 0)
    return jnp.pad(leading, after_pad) + jnp.pad(spread_tail, before_pad)


def along_z(field_in, matrix):
    layout = field_in.shape
    block_size = matrix.shape[0]
    pieces = field_in.reshape(layout[:-1] + (layout[-1] // block_size, block_size))
    return jnp.matmul(pieces, matrix, precision=highest).reshape(layout)


def element_forces(element_vals, lam_w, mu_w, derivative, z_grad, z_back):
    grad_x = jnp.einsum("pi,cxiyjz->cxpyjz", derivative, element_vals, precision=highest)
    grad_y = jnp.einsum("pj,cxiyjz->cxiypz", derivative, element_vals, precision=highest)
    grad_z = along_z(element_vals, z_grad)
    gradients = jnp.stack([grad_x, grad_y, grad_z])
    divergence = gradients[0, 0] + gradients[1, 1] + gradients[2, 2]
    identity = jnp.eye(3, dtype=jnp.float32).reshape(3, 3, 1, 1, 1, 1, 1)
    stress = mu_w * (gradients + jnp.swapaxes(gradients, 0, 1)) + lam_w * divergence * identity
    forces = jnp.einsum("pi,cxpyjz->cxiyjz", derivative, stress[0], precision=highest)
    forces = forces + jnp.einsum("pj,cxiypz->cxiyjz", derivative, stress[1], precision=highest)
    return forces + along_z(stress[2], z_back)


def element_diagonal(lam_w, mu_w, ratio_x, ratio_y, ratio_z):
    ratio_sum = ratio_x + ratio_y + ratio_z
    pieces = [
        lam_w * own_ratio + mu_w * (ratio_sum + own_ratio)
        for own_ratio in (ratio_x, ratio_y, ratio_z)
    ]
    return jnp.stack(pieces)


def point_coeffs(lam_el, mu_el, point_w):
    lam_rep = jnp.repeat(lam_el, DEG + 1, axis=2)[:, None, :, None, :]
    mu_rep = jnp.repeat(mu_el, DEG + 1, axis=2)[:, None, :, None, :]
    return (lam_rep * point_w, mu_rep * point_w)


def lame_fields(material, lame):
    labels = jnp.arange(lame.shape[1], dtype=jnp.int32)
    onehot = (material[..., None] == labels).astype(jnp.float32)
    coeffs = jnp.einsum("xyzm,km->kxyz", onehot, lame, precision=highest)
    return (coeffs[0], coeffs[1])


def gather_near(field_in):
    next_x = from_behind(field_in[:, :1], "gx", -1)
    wider_x = jnp.concatenate([field_in, next_x], 1)
    next_y = from_behind(wider_x[:, :, :1], "gy", -1)
    return jnp.concatenate([wider_x, next_y], 2)


def return_sums(partial_value, width_x, width_y):
    from_y = from_behind(partial_value[:, :, width_y:], "gy", 1)
    part_y = partial_value[:, :, :width_y].at[:, :, :1].add(from_y)
    from_x = from_behind(part_y[:, width_x:], "gx", 1)
    return part_y[:, :width_x].at[:, :1].add(from_x)


def local(right_side, guess, material, lame, upper, lower_ratio):
    elems_x, elems_y, elems_z = material.shape
    nodes_x = DEG * elems_x
    nodes_y = DEG * elems_y
    nodes_z = DEG * elems_z - 1
    shape_four = (3, nodes_x, nodes_y, nodes_z)
    source = right_side.reshape(shape_four)
    solution = guess.reshape(shape_four)
    weights_np, derivative_np, ratio_np = gll_tables(DEG)
    weights = jnp.asarray(weights_np, dtype=jnp.float32)
    derivative = jnp.asarray(derivative_np, dtype=jnp.float32)
    stiff_ratio = jnp.asarray(ratio_np, dtype=jnp.float32)
    block_size = min(128, (DEG + 1) * elems_z)
    z_grad = jnp.asarray(
        np.kron(np.eye(block_size // (DEG + 1)), derivative_np.T), dtype=jnp.float32
    )
    z_back = jnp.asarray(np.kron(np.eye(block_size // (DEG + 1)), derivative_np), dtype=jnp.float32)
    gather_z = jnp.asarray(clamped_gather(elems_z), dtype=jnp.float32)
    gather_t = jnp.asarray(clamped_gather(elems_z).T, dtype=jnp.float32)
    weights_z = jnp.tile(weights, elems_z)
    point_w = (
        weights[None, :, None, None, None]
        * weights[None, None, None, :, None]
        * weights_z[None, None, None, None, :]
    )
    ratio_x = stiff_ratio.reshape(1, DEG + 1, 1, 1, 1)
    ratio_y = stiff_ratio.reshape(1, 1, 1, DEG + 1, 1)
    ratio_z = jnp.tile(stiff_ratio, elems_z).reshape(1, 1, 1, 1, -1)

    def local_operator(extended, lam_w, mu_w):
        z_local = jnp.matmul(extended, gather_z, precision=highest)
        element_vals = split_open(split_open(z_local, 1), 3)
        forces = element_forces(element_vals, lam_w, mu_w, derivative, z_grad, z_back)
        return jnp.matmul(fold_open(fold_open(forces, 3), 1), gather_t, precision=highest)

    lam_el, mu_el = lame_fields(material, lame)
    lam_w, mu_w = point_coeffs(lam_el, mu_el, point_w)
    pieces = element_diagonal(lam_w, mu_w, ratio_x, ratio_y, ratio_z)
    diagonal = return_sums(
        jnp.matmul(fold_open(fold_open(pieces, 3), 1), gather_t, precision=highest),
        nodes_x,
        nodes_y,
    )

    def apply_operator(field_in):
        partial_value = local_operator(gather_near(field_in), lam_w, mu_w)
        return return_sums(partial_value, nodes_x, nodes_y)

    inverse = 1.0 / diagonal
    upper_edge = upper[0]
    lower_edge = lower_ratio[0] * upper_edge
    center = (upper_edge + lower_edge) / 2.0
    radius = (upper_edge - lower_edge) / 2.0
    sigma_ratio = center / radius
    for sweep_index in range(SWEEPS):
        residual = source - apply_operator(solution)
        change = inverse * residual / center
        solution = solution + change
        factor = 1.0 / sigma_ratio
        for step_index in range(CHEB - 1):
            factor_next = 1.0 / (2.0 * sigma_ratio - factor)
            residual = source - apply_operator(solution)
            change = factor_next * factor * change + 2.0 * factor_next / radius * inverse * residual
            solution = solution + change
            factor = factor_next
    residual = source - apply_operator(solution)
    flat_shape = (3, nodes_x, nodes_y * nodes_z)
    return (solution.reshape(flat_shape), residual.reshape(flat_shape))


def solution(mesh):
    placed = (P(None, "gx", "gy"), P(None, "gx", "gy"), P("gx", "gy", None), P(), P(), P())
    return jax.shard_map(
        local,
        mesh=mesh,
        in_specs=placed,
        out_specs=(P(None, "gx", "gy"), P(None, "gx", "gy")),
        check_vma=False,
    )
```

profile of v0, /device:TPU:0, one launch (start us, length us, event | category | flops | bytes accessed | tf_op | source)
XLA Modules:
  0.0 316.3 jit_solution(294162492709428571)
XLA Ops:
  0.7 3.6 %reshape.920 = f32[3,28,28,111]{3,2,1,0:T(8,128)S(1)} reshape(f32[3,28,3108]{2,1,0:T(8,128)} %param.46) | data formatting | bytes 2088576 | tf_op jit(solution)/shard_map/reshape | solution.py:147
  4.9 6.0 %collective-permute-start.2 = (f32[3,1,28,111]{3,2,1,0:T(8,128)}, f32[3,1,28,111]{3,2,1,0:T(8,128)}, u32[]{:S(2)}, u32[]{:S(2)}) collective-permute-start(f32[3,1,28,111]{3,2,1,0:T(8,128)} %slice.1107), channel_id=1, source_target_pairs={{0,28},{4,0},{8,4},{12,8},{16,12},{20,16},{24,20},{28,24},{1,29},{... | collective-permute-start | bytes 111896 | tf_op jit(solution)/shard_map/ppermute | solution.py:17
  18.0 2.0 collective-permute-start.3
  21.3 2.3 reshape.925
  23.7 2.7 fusion.63
  40.2 2.2 fusion.34
  47.8 1.9 scatter-add.54
  53.7 1.9 scatter-add.56
  56.3 3.3 %collective-permute-done.1 = f32[3,1,28,111]{3,2,1,0:T(8,128)} collective-permute-done((f32[3,1,28,111]{3,2,1,0:T(8,128)}, f32[3,1,28,111]{3,2,1,0:T(8,128)}, u32[]{:S(2)}, u32[]{:S(2)}) %collective-permute-start.1) | collective-permute-done | bytes 37328 | tf_op jit(solution)/shard_map/ppermute | solution.py:17
  65.0 2.2 collective-permute-start.6
  67.2 1.9 collective-permute-done.6
  85.6 2.2 fusion.33
  94.0 1.9 scatter-add.60
  99.1 5.5 %collective-permute-done.9 = f32[3,1,28,111]{3,2,1,0:T(8,128)} collective-permute-done((f32[3,1,28,111]{3,2,1,0:T(8,128)}, f32[3,1,28,111]{3,2,1,0:T(8,128)}, u32[]{:S(2)}, u32[]{:S(2)}) %collective-permute-start.9) | collective-permute-done | bytes 37328 | tf_op jit(solution)/shard_map/ppermute | solution.py:17
  106.7 2.0 collective-permute-start.10
  108.7 2.1 collective-permute-done.10
  125.3 2.0 fusion.51
  127.3 2.2 fusion.32
  135.7 1.9 scatter-add.64
  140.7 5.4 %collective-permute-done.13 = f32[3,1,28,111]{3,2,1,0:T(8,128)} collective-permute-done((f32[3,1,28,111]{3,2,1,0:T(8,128)}, f32[3,1,28,111]{3,2,1,0:T(8,128)}, u32[]{:S(2)}, u32[]{:S(2)}) %collective-permute-start.13) | collective-permute-done | bytes 37328 | tf_op jit(solution)/shard_map/ppermute | solution.py:17
  147.0 2.4 add_add_fusion.1
  149.4 2.1 collective-permute-start.14
  151.4 2.1 collective-permute-done.14
  169.8 2.2 fusion.31
  176.3 1.8 collective-permute-done.16
  178.2 1.9 scatter-add.66
  182.5 5.2 %collective-permute-done.17 = f32[3,1,28,111]{3,2,1,0:T(8,128)S(1)} collective-permute-done((f32[3,1,28,111]{3,2,1,0:T(8,128)S(1)}, f32[3,1,28,111]{3,2,1,0:T(8,128)S(1)}, u32[]{:S(2)}, u32[]{:S(2)}) %collective-permute-start.17) | collective-permute-done | bytes 37328 | tf_op jit(solution)/shard_map/ppermute | solution.py:17
  189.6 2.0 collective-permute-start.18
  191.6 2.1 collective-permute-done.18
  210.2 2.2 fusion.30
  216.6 1.8 collective-permute-done.20
  218.5 1.9 scatter-add.70
  222.9 5.2 %collective-permute-done.21 = f32[3,1,28,111]{3,2,1,0:T(8,128)S(1)} collective-permute-done((f32[3,1,28,111]{3,2,1,0:T(8,128)S(1)}, f32[3,1,28,111]{3,2,1,0:T(8,128)S(1)}, u32[]{:S(2)}, u32[]{:S(2)}) %collective-permute-start.21) | collective-permute-done | bytes 37328 | tf_op jit(solution)/shard_map/ppermute | solution.py:17
  230.1 2.0 collective-permute-start.22
  232.2 2.1 collective-permute-done.22
  248.8 2.0 fusion.39
  250.8 2.2 fusion.29
  257.2 1.8 collective-permute-done.24
  259.1 1.9 scatter-add.74
  263.5 5.2 %collective-permute-done.25 = f32[3,1,28,111]{3,2,1,0:T(8,128)S(1)} collective-permute-done((f32[3,1,28,111]{3,2,1,0:T(8,128)S(1)}, f32[3,1,28,111]{3,2,1,0:T(8,128)S(1)}, u32[]{:S(2)}, u32[]{:S(2)}) %collective-permute-start.25) | collective-permute-done | bytes 37328 | tf_op jit(solution)/shard_map/ppermute | solution.py:17
  269.5 2.4 add_add_fusion
  271.9 2.1 collective-permute-start.26
  273.9 2.1 collective-permute-done.26
  292.3 2.3 fusion.28
  300.8 1.9 scatter-add.76
  303.5 2.3 reshape.968
  307.2 3.1 collective-permute-done.29
  312.5 3.6 %reshape.976 = f32[3,28,3108]{2,1,0:T(8,128)} reshape(f32[3,28,28,111]{3,2,1,0:T(8,128)} %sub.41) | data formatting | bytes 2088576 | tf_op jit(solution)/shard_map/reshape | solution.py:207
  (417 shorter events, 186.3 us)
Async XLA Ops:
  0.6 10.7 %copy-start = (f32[2,8]{1,0:T(2,128)S(1)}, f32[2,8]{1,0:T(2,128)}, u32[]{:S(2)}) copy-start(f32[2,8]{1,0:T(2,128)} %param.48) | copy-start | bytes 196
  0.6 10.3 %copy-start.49 = (f32[8]{0:T(128)S(1)}, f32[8]{0:T(128)}, u32[]{:S(2)}) copy-start(f32[8]{0:T(128)} %constant.357.clone) | copy-start | bytes 100
  0.7 10.4 %copy-start.48 = (f32[8]{0:T(128)S(1)}, f32[8]{0:T(128)}, u32[]{:S(2)}) copy-start(f32[8]{0:T(128)} %constant.359.clone) | copy-start | bytes 100
  0.7 10.6 %copy-start.50 = (s32[4,4,16]{2,1,0:T(4,128)S(1)}, s32[4,4,16]{2,1,0:T(4,128)}, u32[]{:S(2)}) copy-start(s32[4,4,16]{2,1,0:T(4,128)} %param.47) | copy-start | bytes 3076
  4.3 12.6 %copy-start.6 = (f32[3,28,28,111]{3,2,1,0:T(8,128)}, f32[3,28,28,111]{3,2,1,0:T(8,128)S(1)}, u32[]{:S(2)}) copy-start(f32[3,28,28,111]{3,2,1,0:T(8,128)S(1)} %reshape.920) | copy-start | bytes 3132868
  4.9 12.1 %collective-permute-start.2 = (f32[3,1,28,111]{3,2,1,0:T(8,128)}, f32[3,1,28,111]{3,2,1,0:T(8,128)}, u32[]{:S(2)}, u32[]{:S(2)}) collective-permute-start(f32[3,1,28,111]{3,2,1,0:T(8,128)} %slice.1107), channel_id=1, source_target_pairs={{0,28},{4,0},{8,4},{12,8},{16,12},{20,16},{24,20},{28,24},{1,29},{... | collective-permute-start | bytes 111896 | tf_op jit(solution)/shard_map/ppermute | solution.py:17
  16.8 29.9 %collective-permute-start = (f32[3,29,1,111]{3,2,1,0:T(1,128)}, f32[3,29,1,111]{3,2,1,0:T(1,128)S(1)}, u32[]{:S(2)}, u32[]{:S(2)}) collective-permute-start(f32[3,29,1,111]{3,2,1,0:T(1,128)} %slice.1103), channel_id=1, source_target_pairs={{0,1},{1,2},{2,3},{3,0},{4,5},{5,6},{6,7},{7,4},{8,9},{9,10},{10,1... | collective-permute-start | bytes 115892 | tf_op jit(solution)/shard_map/ppermute | solution.py:17
  18.0 5.6 %collective-permute-start.3 = (f32[3,29,1,111]{3,2,1,0:T(1,128)S(1)}, f32[3,29,1,111]{3,2,1,0:T(1,128)S(1)}, u32[]{:S(2)}, u32[]{:S(2)}) collective-permute-start(f32[3,29,1,111]{3,2,1,0:T(1,128)S(1)} %slice.1108), channel_id=1, source_target_pairs={{0,3},{1,0},{2,1},{3,2},{4,7},{5,4},{6,5},{7,6},{8,11},{9,8},{10,9... | collective-permute-start | bytes 115892 | tf_op jit(solution)/shard_map/ppermute | solution.py:17
  20.0 15.0 %copy-start.41 = (f32[3,3]{1,0:T(4,128)}, f32[3,3]{1,0:T(4,128)S(1)}, u32[]{:S(2)}) copy-start(f32[3,3]{1,0:T(4,128)S(1)} %fusion.170) | copy-start | bytes 112
  46.7 5.9 %collective-permute-start.4 = (f32[3,29,1,111]{3,2,1,0:T(1,128)}, f32[3,29,1,111]{3,2,1,0:T(1,128)}, u32[]{:S(2)}, u32[]{:S(2)}) collective-permute-start(f32[3,29,1,111]{3,2,1,0:T(1,128)} %slice.1124), channel_id=1, source_target_pairs={{0,1},{1,2},{2,3},{3,0},{4,5},{5,6},{6,7},{7,4},{8,9},{9,10},{10,1... | collective-permute-start | bytes 115892 | tf_op jit(solution)/shard_map/ppermute | solution.py:17
  52.5 7.2 %collective-permute-start.1 = (f32[3,1,28,111]{3,2,1,0:T(8,128)}, f32[3,1,28,111]{3,2,1,0:T(8,128)}, u32[]{:S(2)}, u32[]{:S(2)}) collective-permute-start(f32[3,1,28,111]{3,2,1,0:T(8,128)} %slice.1106), channel_id=1, source_target_pairs={{0,4},{4,8},{8,12},{12,16},{16,20},{20,24},{24,28},{28,0},{1,5},{5... | collective-permute-start | bytes 111896 | tf_op jit(solution)/shard_map/ppermute | solution.py:17
  56.3 6.8 %collective-permute-start.5 = (f32[3,1,28,111]{3,2,1,0:T(8,128)S(1)}, f32[3,1,28,111]{3,2,1,0:T(8,128)S(1)}, u32[]{:S(2)}, u32[]{:S(2)}) collective-permute-start(f32[3,1,28,111]{3,2,1,0:T(8,128)S(1)} %slice.1127), channel_id=1, source_target_pairs={{0,4},{4,8},{8,12},{12,16},{16,20},{20,24},{24,28},{28,0},{1,5},{5... | collective-permute-start | bytes 111896 | tf_op jit(solution)/shard_map/ppermute | solution.py:17
  65.0 4.1 %collective-permute-start.6 = (f32[3,1,28,111]{3,2,1,0:T(8,128)S(1)}, f32[3,1,28,111]{3,2,1,0:T(8,128)S(1)}, u32[]{:S(2)}, u32[]{:S(2)}) collective-permute-start(f32[3,1,28,111]{3,2,1,0:T(8,128)S(1)} %slice.1128), channel_id=1, source_target_pairs={{0,28},{4,0},{8,4},{12,8},{16,12},{20,16},{24,20},{28,24},{1,29},{... | collective-permute-start | bytes 111896 | tf_op jit(solution)/shard_map/ppermute | solution.py:17
  69.2 2.2 collective-permute-start.7
  90.4 3.5 %collective-permute-start.8 = (f32[3,29,1,111]{3,2,1,0:T(1,128)S(1)}, f32[3,29,1,111]{3,2,1,0:T(1,128)S(1)}, u32[]{:S(2)}, u32[]{:S(2)}) collective-permute-start(f32[3,29,1,111]{3,2,1,0:T(1,128)S(1)} %slice.1144), channel_id=1, source_target_pairs={{0,1},{1,2},{2,3},{3,0},{4,5},{5,6},{6,7},{7,4},{8,9},{9,10},{10,1... | collective-permute-start | bytes 115892 | tf_op jit(solution)/shard_map/ppermute | solution.py:17
  97.3 7.3 %collective-permute-start.9 = (f32[3,1,28,111]{3,2,1,0:T(8,128)}, f32[3,1,28,111]{3,2,1,0:T(8,128)}, u32[]{:S(2)}, u32[]{:S(2)}) collective-permute-start(f32[3,1,28,111]{3,2,1,0:T(8,128)} %slice.1147), channel_id=1, source_target_pairs={{0,4},{4,8},{8,12},{12,16},{16,20},{20,24},{24,28},{28,0},{1,5},{5... | collective-permute-start | bytes 111896 | tf_op jit(solution)/shard_map/ppermute | solution.py:17
  97.5 7.9 %copy-start.8 = (f32[3,28,28,111]{3,2,1,0:T(8,128)S(1)}, f32[3,28,28,111]{3,2,1,0:T(8,128)}, u32[]{:S(2)}) copy-start(f32[3,28,28,111]{3,2,1,0:T(8,128)} %copy-done.6) | copy-start | bytes 3132868
  97.5 7.9 %copy-start.13 = (f32[3,28,28,111]{3,2,1,0:T(8,128)S(1)}, f32[3,28,28,111]{3,2,1,0:T(8,128)}, u32[]{:S(2)}) copy-start(f32[3,28,28,111]{3,2,1,0:T(8,128)} %copy-done.12) | copy-start | bytes 3132868
  106.7 4.1 %collective-permute-start.10 = (f32[3,1,28,111]{3,2,1,0:T(8,128)S(1)}, f32[3,1,28,111]{3,2,1,0:T(8,128)S(1)}, u32[]{:S(2)}, u32[]{:S(2)}) collective-permute-start(f32[3,1,28,111]{3,2,1,0:T(8,128)S(1)} %slice.1148), channel_id=1, source_target_pairs={{0,28},{4,0},{8,4},{12,8},{16,12},{20,16},{24,20},{28,24},{1,29},{... | collective-permute-start | bytes 111896 | tf_op jit(solution)/shard_map/ppermute | solution.py:17
  110.8 2.0 collective-permute-start.11
  132.1 3.5 %collective-permute-start.12 = (f32[3,29,1,111]{3,2,1,0:T(1,128)S(1)}, f32[3,29,1,111]{3,2,1,0:T(1,128)S(1)}, u32[]{:S(2)}, u32[]{:S(2)}) collective-permute-start(f32[3,29,1,111]{3,2,1,0:T(1,128)S(1)} %slice.1164), channel_id=1, source_target_pairs={{0,1},{1,2},{2,3},{3,0},{4,5},{5,6},{6,7},{7,4},{8,9},{9,10},{10,1... | collective-permute-start | bytes 115892 | tf_op jit(solution)/shard_map/ppermute | solution.py:17
  139.0 7.1 %collective-permute-start.13 = (f32[3,1,28,111]{3,2,1,0:T(8,128)}, f32[3,1,28,111]{3,2,1,0:T(8,128)}, u32[]{:S(2)}, u32[]{:S(2)}) collective-permute-start(f32[3,1,28,111]{3,2,1,0:T(8,128)} %slice.1167), channel_id=1, source_target_pairs={{0,4},{4,8},{8,12},{12,16},{16,20},{20,24},{24,28},{28,0},{1,5},{5... | collective-permute-start | bytes 111896 | tf_op jit(solution)/shard_map/ppermute | solution.py:17
  139.1 7.8 %copy-start.9 = (f32[3,28,28,111]{3,2,1,0:T(8,128)S(1)}, f32[3,28,28,111]{3,2,1,0:T(8,128)}, u32[]{:S(2)}) copy-start(f32[3,28,28,111]{3,2,1,0:T(8,128)} %copy-done.6) | copy-start | bytes 3132868
  139.1 7.8 %copy-start.14 = (f32[3,28,28,111]{3,2,1,0:T(8,128)S(1)}, f32[3,28,28,111]{3,2,1,0:T(8,128)}, u32[]{:S(2)}) copy-start(f32[3,28,28,111]{3,2,1,0:T(8,128)} %copy-done.12) | copy-start | bytes 3132868
  149.3 7.5 %copy-start.2 = (f32[3,28,28,111]{3,2,1,0:T(8,128)}, f32[3,28,28,111]{3,2,1,0:T(8,128)S(1)}, u32[]{:S(2)}) copy-start(f32[3,28,28,111]{3,2,1,0:T(8,128)S(1)} %add_add_fusion.1) | copy-start | bytes 3132868
  149.4 4.1 %collective-permute-start.14 = (f32[3,1,28,111]{3,2,1,0:T(8,128)S(1)}, f32[3,1,28,111]{3,2,1,0:T(8,128)S(1)}, u32[]{:S(2)}, u32[]{:S(2)}) collective-permute-start(f32[3,1,28,111]{3,2,1,0:T(8,128)S(1)} %slice.1168), channel_id=1, source_target_pairs={{0,28},{4,0},{8,4},{12,8},{16,12},{20,16},{24,20},{28,24},{1,29},{... | collective-permute-start | bytes 111896 | tf_op jit(solution)/shard_map/ppermute | solution.py:17
  153.6 1.9 collective-permute-start.15
  174.6 3.5 %collective-permute-start.16 = (f32[3,29,1,111]{3,2,1,0:T(1,128)S(1)}, f32[3,29,1,111]{3,2,1,0:T(1,128)S(1)}, u32[]{:S(2)}, u32[]{:S(2)}) collective-permute-start(f32[3,29,1,111]{3,2,1,0:T(1,128)S(1)} %slice.1184), channel_id=1, source_target_pairs={{0,1},{1,2},{2,3},{3,0},{4,5},{5,6},{6,7},{7,4},{8,9},{9,10},{10,1... | collective-permute-start | bytes 115892 | tf_op jit(solution)/shard_map/ppermute | solution.py:17
  180.9 7.6 %copy-start.3 = (f32[3,28,28,111]{3,2,1,0:T(8,128)S(1)}, f32[3,28,28,111]{3,2,1,0:T(8,128)}, u32[]{:S(2)}) copy-start(f32[3,28,28,111]{3,2,1,0:T(8,128)} %copy-done.2) | copy-start | bytes 3132868
  180.9 6.8 %collective-permute-start.17 = (f32[3,1,28,111]{3,2,1,0:T(8,128)S(1)}, f32[3,1,28,111]{3,2,1,0:T(8,128)S(1)}, u32[]{:S(2)}, u32[]{:S(2)}) collective-permute-start(f32[3,1,28,111]{3,2,1,0:T(8,128)S(1)} %slice.1187), channel_id=1, source_target_pairs={{0,4},{4,8},{8,12},{12,16},{16,20},{20,24},{24,28},{28,0},{1,5},{5... | collective-permute-start | bytes 111896 | tf_op jit(solution)/shard_map/ppermute | solution.py:17
  189.6 4.1 %collective-permute-start.18 = (f32[3,1,28,111]{3,2,1,0:T(8,128)S(1)}, f32[3,1,28,111]{3,2,1,0:T(8,128)S(1)}, u32[]{:S(2)}, u32[]{:S(2)}) collective-permute-start(f32[3,1,28,111]{3,2,1,0:T(8,128)S(1)} %slice.1188), channel_id=1, source_target_pairs={{0,28},{4,0},{8,4},{12,8},{16,12},{20,16},{24,20},{28,24},{1,29},{... | collective-permute-start | bytes 111896 | tf_op jit(solution)/shard_map/ppermute | solution.py:17
  193.7 2.2 collective-permute-start.19
  214.9 3.5 %collective-permute-start.20 = (f32[3,29,1,111]{3,2,1,0:T(1,128)S(1)}, f32[3,29,1,111]{3,2,1,0:T(1,128)S(1)}, u32[]{:S(2)}, u32[]{:S(2)}) collective-permute-start(f32[3,29,1,111]{3,2,1,0:T(1,128)S(1)} %slice.1204), channel_id=1, source_target_pairs={{0,1},{1,2},{2,3},{3,0},{4,5},{5,6},{6,7},{7,4},{8,9},{9,10},{10,1... | collective-permute-start | bytes 115892 | tf_op jit(solution)/shard_map/ppermute | solution.py:17
  221.3 7.6 %copy-start.4 = (f32[3,28,28,111]{3,2,1,0:T(8,128)S(1)}, f32[3,28,28,111]{3,2,1,0:T(8,128)}, u32[]{:S(2)}) copy-start(f32[3,28,28,111]{3,2,1,0:T(8,128)} %copy-done.2) | copy-start | bytes 3132868
  221.3 7.6 %copy-start.16 = (f32[3,28,28,111]{3,2,1,0:T(8,128)S(1)}, f32[3,28,28,111]{3,2,1,0:T(8,128)}, u32[]{:S(2)}) copy-start(f32[3,28,28,111]{3,2,1,0:T(8,128)} %copy-done.15) | copy-start | bytes 3132868
  221.3 6.8 %collective-permute-start.21 = (f32[3,1,28,111]{3,2,1,0:T(8,128)S(1)}, f32[3,1,28,111]{3,2,1,0:T(8,128)S(1)}, u32[]{:S(2)}, u32[]{:S(2)}) collective-permute-start(f32[3,1,28,111]{3,2,1,0:T(8,128)S(1)} %slice.1207), channel_id=1, source_target_pairs={{0,4},{4,8},{8,12},{12,16},{16,20},{20,24},{24,28},{28,0},{1,5},{5... | collective-permute-start | bytes 111896 | tf_op jit(solution)/shard_map/ppermute | solution.py:17
  230.1 4.1 %collective-permute-start.22 = (f32[3,1,28,111]{3,2,1,0:T(8,128)S(1)}, f32[3,1,28,111]{3,2,1,0:T(8,128)S(1)}, u32[]{:S(2)}, u32[]{:S(2)}) collective-permute-start(f32[3,1,28,111]{3,2,1,0:T(8,128)S(1)} %slice.1208), channel_id=1, source_target_pairs={{0,28},{4,0},{8,4},{12,8},{16,12},{20,16},{24,20},{28,24},{1,29},{... | collective-permute-start | bytes 111896 | tf_op jit(solution)/shard_map/ppermute | solution.py:17
  234.3 2.0 collective-permute-start.23
  255.5 3.5 %collective-permute-start.24 = (f32[3,29,1,111]{3,2,1,0:T(1,128)S(1)}, f32[3,29,1,111]{3,2,1,0:T(1,128)S(1)}, u32[]{:S(2)}, u32[]{:S(2)}) collective-permute-start(f32[3,29,1,111]{3,2,1,0:T(1,128)S(1)} %slice.1224), channel_id=1, source_target_pairs={{0,1},{1,2},{2,3},{3,0},{4,5},{5,6},{6,7},{7,4},{8,9},{9,10},{10,1... | collective-permute-start | bytes 115892 | tf_op jit(solution)/shard_map/ppermute | solution.py:17
  261.8 7.6 %copy-start.5 = (f32[3,28,28,111]{3,2,1,0:T(8,128)S(1)}, f32[3,28,28,111]{3,2,1,0:T(8,128)}, u32[]{:S(2)}) copy-start(f32[3,28,28,111]{3,2,1,0:T(8,128)} %copy-done.2) | copy-start | bytes 3132868
  261.8 7.6 %copy-start.17 = (f32[3,28,28,111]{3,2,1,0:T(8,128)S(1)}, f32[3,28,28,111]{3,2,1,0:T(8,128)}, u32[]{:S(2)}) copy-start(f32[3,28,28,111]{3,2,1,0:T(8,128)} %copy-done.15) | copy-start | bytes 3132868
  261.8 6.8 %collective-permute-start.25 = (f32[3,1,28,111]{3,2,1,0:T(8,128)S(1)}, f32[3,1,28,111]{3,2,1,0:T(8,128)S(1)}, u32[]{:S(2)}, u32[]{:S(2)}) collective-permute-start(f32[3,1,28,111]{3,2,1,0:T(8,128)S(1)} %slice.1227), channel_id=1, source_target_pairs={{0,4},{4,8},{8,12},{12,16},{16,20},{20,24},{24,28},{28,0},{1,5},{5... | collective-permute-start | bytes 111896 | tf_op jit(solution)/shard_map/ppermute | solution.py:17
  271.8 7.5 %copy-start.10 = (f32[3,28,28,111]{3,2,1,0:T(8,128)}, f32[3,28,28,111]{3,2,1,0:T(8,128)S(1)}, u32[]{:S(2)}) copy-start(f32[3,28,28,111]{3,2,1,0:T(8,128)S(1)} %add_add_fusion) | copy-start | bytes 3132868
  271.9 4.1 %collective-permute-start.26 = (f32[3,1,28,111]{3,2,1,0:T(8,128)S(1)}, f32[3,1,28,111]{3,2,1,0:T(8,128)S(1)}, u32[]{:S(2)}, u32[]{:S(2)}) collective-permute-start(f32[3,1,28,111]{3,2,1,0:T(8,128)S(1)} %slice.1228), channel_id=1, source_target_pairs={{0,28},{4,0},{8,4},{12,8},{16,12},{20,16},{24,20},{28,24},{1,29},{... | collective-permute-start | bytes 111896 | tf_op jit(solution)/shard_map/ppermute | solution.py:17
  276.0 1.9 collective-permute-start.27
  295.8 7.7 %copy-start.11 = (f32[3,28,28,111]{3,2,1,0:T(8,128)S(1)}, f32[3,28,28,111]{3,2,1,0:T(8,128)}, u32[]{:S(2)}) copy-start(f32[3,28,28,111]{3,2,1,0:T(8,128)} %copy-done.10) | copy-start | bytes 3132868
  297.2 3.5 %collective-permute-start.28 = (f32[3,29,1,111]{3,2,1,0:T(1,128)S(1)}, f32[3,29,1,111]{3,2,1,0:T(1,128)S(1)}, u32[]{:S(2)}, u32[]{:S(2)}) collective-permute-start(f32[3,29,1,111]{3,2,1,0:T(1,128)S(1)} %slice.1244), channel_id=1, source_target_pairs={{0,1},{1,2},{2,3},{3,0},{4,5},{5,6},{6,7},{7,4},{8,9},{9,10},{10,1... | collective-permute-start | bytes 115892 | tf_op jit(solution)/shard_map/ppermute | solution.py:17
  303.5 6.8 %collective-permute-start.29 = (f32[3,1,28,111]{3,2,1,0:T(8,128)S(1)}, f32[3,1,28,111]{3,2,1,0:T(8,128)S(1)}, u32[]{:S(2)}, u32[]{:S(2)}) collective-permute-start(f32[3,1,28,111]{3,2,1,0:T(8,128)S(1)} %slice.1247), channel_id=1, source_target_pairs={{0,4},{4,8},{8,12},{12,16},{16,20},{20,24},{24,28},{28,0},{1,5},{5... | collective-permute-start | bytes 111896 | tf_op jit(solution)/shard_map/ppermute | solution.py:17
  (33 other events, 95.7 us)
where the time goes:
time: 322 us; the launch traced here: 316 us
  matrix products  90.8 us (28%)
  local copies, waits for them, and re-layouts  80.8 us (25%)
  waiting for transfers between devices  67.3 us (21%)
  other arithmetic  39.8 us (12%)
  starting transfers between devices  32.7 us (10%)
  between operations  4.9 us (2%)
    ppermute x30, waiting for transfers between devices, from_behind(): lax.ppermute(value, axis, [(i, (i + by) % size) for i in range(size)])  67.3 us
    ppermute x30, starting transfers between devices, from_behind(): lax.ppermute(value, axis, [(i, (i + by) % size) for i in range(size)])  32.7 us
    dot_general x14, matrix products, along_z(): return jnp.matmul(pieces, matrix, precision=highest).reshape(layout)  20 us
    dot_general x7, matrix products, element_forces(): jnp.einsum('pi,cxpyjz->cxiyjz', derivative, stress[0], precision=highest)  15.8 us
    scatter-add x8, local copies, waits for them, and re-layouts, return_sums(): part_y = partial_value[:, :, :width_y].at[:, :, :1].add(from_y)  15.2 us
    dot_general x7, matrix products, element_forces(): jnp.einsum('pj,cxiypz->cxiyjz', derivative, stress[1], precision=highest)  12.7 us
    slice x8, local copies, waits for them, and re-layouts, return_sums(): return part_y[:, :width_x].at[:, :1].add(from_x)  12.4 us
    dot_general x7, matrix products, element_forces(): jnp.einsum('pj,cxiyjz->cxiypz', derivative, element_vals, precision=highest)  11.1 us
  transfers between devices with their start and end apart: 30, of which 26 were waited for; matrix products, arithmetic and copies ran while one was open for 17% of the time, Pallas kernels for 0%

commit v1 on v0

v1 whole, which is shorter than its diff:
```python
import jax
import jax.numpy as jnp
import numpy as np
from jax import lax
from jax.experimental import pallas as pl
from jax.experimental.pallas import tpu as pltpu
from jax.sharding import PartitionSpec as P

DEG = 7
SWEEPS = 2
CHEB = 3


highest = lax.Precision.HIGHEST


def legendre_pair(points, degree):
    prev_poly = points * 0.0 + 1.0
    this_poly = points * 1.0
    for order in range(2, degree + 1):
        next_poly = ((2 * order - 1) * points * this_poly - (order - 1) * prev_poly) / order
        prev_poly = this_poly
        this_poly = next_poly
    return (this_poly, prev_poly)


def gll_tables(degree):
    count = degree + 1
    points = -np.cos(np.pi * np.arange(count) / degree)
    for newton_step in range(60):
        this_poly, prev_poly = legendre_pair(points, degree)
        points = points - (points * this_poly - prev_poly) / (count * this_poly)
    values, unused_poly = legendre_pair(points, degree)
    weights = 2.0 / (degree * (degree + 1) * values**2)
    identity_np = np.eye(count)
    spacing = points[:, None] - points[None, :] + identity_np
    derivative = values[:, None] / (values[None, :] * spacing) * (1.0 - identity_np)
    derivative[0, 0] = -degree * (degree + 1) / 4.0
    derivative[degree, degree] = degree * (degree + 1) / 4.0
    stiff_ratio = (weights[:, None] * derivative**2).sum(0) / weights
    return (weights, derivative, stiff_ratio)


def clamped_gather(blocks):
    free_nodes = DEG * blocks - 1
    selector = np.zeros((free_nodes, blocks * (DEG + 1)), np.float32)
    for element in range(blocks):
        for node_idx in range(DEG + 1):
            target = DEG * element + node_idx - 1
            if 0 <= target < free_nodes:
                selector[target, element * (DEG + 1) + node_idx] = 1.0
    return selector


def lame_fields(material, lame):
    labels = jnp.arange(lame.shape[1], dtype=jnp.int32)
    onehot = (material[..., None] == labels).astype(jnp.float32)
    coeffs = jnp.einsum("xyzm,km->kxyz", onehot, lame, precision=highest)
    return (coeffs[0], coeffs[1])


N1 = DEG + 1
SLOTS = 4


def halves(value):
    high = value.astype(jnp.bfloat16)
    low = (value - high.astype(jnp.float32)).astype(jnp.bfloat16)
    return high, low


def np_halves(matrix):
    high = np.asarray(matrix, np.float32).astype(jnp.bfloat16)
    low = (np.asarray(matrix, np.float64) - high.astype(np.float64)).astype(jnp.bfloat16)
    return high, low


def apply_pairs(matrix, values):
    half = N1 // 2
    even = [values[i] + values[DEG - i] for i in range(half)]
    odd = [values[i] - values[DEG - i] for i in range(half)]
    outs = [None] * N1
    for p in range(half):
        plus = None
        minus = None
        for i in range(half):
            by_even = float(np.float32((matrix[p, i] + matrix[p, DEG - i]) / 2))
            by_odd = float(np.float32((matrix[p, i] - matrix[p, DEG - i]) / 2))
            plus = by_even * even[i] if plus is None else plus + by_even * even[i]
            minus = by_odd * odd[i] if minus is None else minus + by_odd * odd[i]
        outs[p] = minus + plus
        outs[DEG - p] = minus - plus
    return outs


def smoother_kernel(
    steps,
    elems_x,
    elems_y,
    derivative,
    coef,
    guess,
    source,
    lam_in,
    mu_in,
    weight_in,
    own_in,
    sum_in,
    grad_in,
    back_in,
    join_in,
    field,
    resid,
    lam_w,
    mu_w,
    inverse,
    change,
    grad_x,
    grad_y,
    grad_z,
    send_x,
    send_y,
    send_c,
    recv_x,
    recv_y,
    recv_c,
    send_sem,
    recv_sem,
):
    cols = elems_x * elems_y
    size_x = lax.axis_size("gx")
    size_y = lax.axis_size("gy")
    me_x = lax.axis_index("gx")
    me_y = lax.axis_index("gy")
    near_x = (lax.rem(me_x + size_x - 1, size_x), lax.rem(me_x + 1, size_x))
    near_y = (lax.rem(me_y + size_y - 1, size_y), lax.rem(me_y + 1, size_y))
    partners = [(near_x[0], me_y), (near_x[1], me_y), (me_x, near_y[0]), (me_x, near_y[1])]
    partners += [(near_x[a], near_y[b]) for a in range(2) for b in range(2)]

    barrier = pltpu.get_barrier_semaphore()
    for partner in partners:
        pl.semaphore_signal(
            barrier, inc=1, device_id=partner, device_id_type=pl.DeviceIdType.MESH
        )
    pl.semaphore_wait(barrier, len(partners))

    def copies(slot):
        made = []
        for d in range(8):
            if d < 2:
                src, dst = send_x.at[slot, d], recv_x.at[slot, 1 - d]
            elif d < 4:
                src, dst = send_y.at[slot, d - 2], recv_y.at[slot, 3 - d]
            else:
                src, dst = send_c.at[slot, d - 4], recv_c.at[slot, 7 - d]
            mirror = (1, 0, 3, 2, 7, 6, 5, 4)[d]
            made.append(
                pltpu.make_async_remote_copy(
                    src_ref=src,
                    dst_ref=dst,
                    send_sem=send_sem.at[slot, d],
                    recv_sem=recv_sem.at[slot, mirror],
                    device_id=partners[d],
                    device_id_type=pl.DeviceIdType.MESH,
                )
            )
        return made

    rows = lax.broadcasted_iota(jnp.int32, (N1 * cols, 128), 0) % cols
    row_y = rows % elems_y
    inner_low_x = rows >= elems_y
    inner_high_x = rows < cols - elems_y
    inner_low_y = row_y >= 1
    inner_high_y = row_y < elems_y - 1

    def local_sum(ref):
        flat = (N1 * cols, 128)
        full = (N1, cols, 128)
        zero = jnp.zeros(flat, jnp.float32)
        for c in range(3):
            low = ref[c, 0].reshape(flat)
            high = ref[c, DEG].reshape(flat)
            to_low = jnp.where(inner_low_x, pltpu.roll(high, elems_y, 0), zero)
            to_high = jnp.where(inner_high_x, pltpu.roll(low, N1 * cols - elems_y, 0), zero)
            ref[c, 0] = (low + to_low).reshape(full)
            ref[c, DEG] = (high + to_high).reshape(full)
        for c in range(3):
            low = ref[c, :, 0].reshape(flat)
            high = ref[c, :, DEG].reshape(flat)
            to_low = jnp.where(inner_low_y, pltpu.roll(high, 1, 0), zero)
            to_high = jnp.where(inner_high_y, pltpu.roll(low, N1 * cols - 1, 0), zero)
            ref[c, :, 0] = (low + to_low).reshape(full)
            ref[c, :, DEG] = (high + to_high).reshape(full)

    last_x = cols - elems_y
    last_y = elems_y - 1

    def post(ref, slot):
        for c in range(3):
            send_x[slot, 0, c] = ref[c, 0, :, 0:elems_y, :]
            send_x[slot, 1, c] = ref[c, DEG, :, last_x:cols, :]
            for a in range(elems_x):
                send_y[slot, 0, c, :, a : a + 1, :] = ref[c, :, 0, a * elems_y : a * elems_y + 1, :]
                at = a * elems_y + last_y
                send_y[slot, 1, c, :, a : a + 1, :] = ref[c, :, DEG, at : at + 1, :]
            for a in range(2):
                for b in range(2):
                    at = a * last_x + b * last_y
                    send_c[slot, 2 * a + b, c] = ref[c, a * DEG, b * DEG, at : at + 1, :]
        for copy in copies(slot):
            copy.start()

    def collect(ref, slot):
        for copy in copies(slot):
            copy.wait()
        for c in range(3):
            ref[c, 0, :, 0:elems_y, :] += recv_x[slot, 0, c]
            ref[c, DEG, :, last_x:cols, :] += recv_x[slot, 1, c]
            for a in range(elems_x):
                at = a * elems_y
                ref[c, :, 0, at : at + 1, :] += recv_y[slot, 0, c, :, a : a + 1, :]
                at = a * elems_y + last_y
                ref[c, :, DEG, at : at + 1, :] += recv_y[slot, 1, c, :, a : a + 1, :]
            for a in range(2):
                for b in range(2):
                    at = a * last_x + b * last_y
                    ref[c, a * DEG, b * DEG, at : at + 1, :] += recv_c[slot, 2 * a + b, c]

    @pl.loop(0, 3 * N1)
    def _(at):
        c = at // N1
        i = at % N1
        field[c, i] = guess[c, i]

    local_sum(field)
    post(field, 0)

    lam_all = lam_in[...]
    mu_all = mu_in[...]

    @pl.loop(0, N1)
    def _(i):
        for j in range(N1):
            lam_w[i, j] = lam_all * weight_in[i, j]
            mu_w[i, j] = mu_all * weight_in[i, j]

    @pl.loop(0, 3 * N1)
    def _(at):
        c = at // N1
        i = at % N1
        pieces = []
        for j in range(N1):
            own = own_in[c, i, j]
            pieces.append(lam_w[i, j] * own + mu_w[i, j] * (sum_in[i, j] + own))
        high, low = halves(jnp.concatenate(pieces, axis=0))
        summed = jnp.dot(
            jnp.concatenate([high, low], axis=1), join_in[...], preferred_element_type=jnp.float32
        )
        inverse[c, i] = summed.reshape(N1, cols, 128)

    local_sum(inverse)
    post(inverse, 1)
    collect(field, 0)
    collect(inverse, 1)

    @pl.loop(0, 3 * N1)
    def _(at):
        c = at // N1
        i = at % N1
        inverse[c, i] = 1.0 / inverse[c, i]
        change[c, i] = jnp.zeros((N1, cols, 128), jnp.float32)

    def operator():
        @pl.loop(0, 3 * N1)
        def _(at):
            c = at // N1
            j = at % N1
            for p, out in enumerate(apply_pairs(derivative, [field[c, i, j] for i in range(N1)])):
                grad_x[c, p, j] = out

        @pl.loop(0, 3 * N1)
        def _(at):
            c = at // N1
            i = at % N1
            for q, out in enumerate(apply_pairs(derivative, [field[c, i, j] for j in range(N1)])):
                grad_y[c, i, q] = out

        @pl.loop(0, 3 * N1 // 2)
        def _(at):
            c = at // (N1 // 2)
            i = at % (N1 // 2)
            high, low = halves(field[c, pl.ds(2 * i, 2)].reshape(2 * N1 * cols, 128))
            both = jnp.dot(
                jnp.concatenate([high, low], axis=1),
                grad_in[...],
                preferred_element_type=jnp.float32,
            )
            grad_z[c, pl.ds(2 * i, 2)] = (both[:, :128] + both[:, 128:]).reshape(2, N1, cols, 128)

        @pl.loop(0, N1)
        def _(i):
            for j in range(N1):
                lam = lam_w[i, j]
                mu = mu_w[i, j]
                d00, d11, d22 = grad_x[0, i, j], grad_y[1, i, j], grad_z[2, i, j]
                base = lam * (d00 + d11 + d22)
                two = mu + mu
                grad_x[0, i, j] = two * d00 + base
                grad_y[1, i, j] = two * d11 + base
                grad_z[2, i, j] = two * d22 + base
                s01 = mu * (grad_x[1, i, j] + grad_y[0, i, j])
                s02 = mu * (grad_x[2, i, j] + grad_z[0, i, j])
                s12 = mu * (grad_y[2, i, j] + grad_z[1, i, j])
                grad_x[1, i, j] = s01
                grad_y[0, i, j] = s01
                grad_x[2, i, j] = s02
                grad_z[0, i, j] = s02
                grad_y[2, i, j] = s12
                grad_z[1, i, j] = s12

        @pl.loop(0, 3 * N1)
        def _(at):
            c = at // N1
            j = at % N1
            for p, out in enumerate(apply_pairs(derivative.T, [grad_x[c, i, j] for i in range(N1)])):
                resid[c, p, j] = out

        @pl.loop(0, 3 * N1)
        def _(at):
            c = at // N1
            i = at % N1
            for q, out in enumerate(apply_pairs(derivative.T, [grad_y[c, i, j] for j in range(N1)])):
                resid[c, i, q] += out

        @pl.loop(0, 3 * N1 // 2)
        def _(at):
            c = at // (N1 // 2)
            i = at % (N1 // 2)
            pick = pl.ds(2 * i, 2)
            parts = halves(resid[c, pick].reshape(2 * N1 * cols, 128))
            parts += halves(grad_z[c, pick].reshape(2 * N1 * cols, 128))
            both = jnp.dot(
                jnp.concatenate(parts, axis=1), back_in[...], preferred_element_type=jnp.float32
            )
            force = (both[:, :128] + both[:, 128:]).reshape(2, N1, cols, 128)
            resid[c, pick] = source[c, pick] - force

    @pl.loop(0, steps + 1)
    def _(step):
        operator()
        local_sum(resid)
        slot = 2 + step % 2
        post(resid, slot)
        collect(resid, slot)

        @pl.when(step < steps)
        def _():
            alpha = coef[0, step]
            beta = coef[1, step]

            @pl.loop(0, 3 * N1)
            def _(at):
                c = at // N1
                i = at % N1
                new = alpha * change[c, i] + beta * (inverse[c, i] * resid[c, i])
                change[c, i] = new
                field[c, i] += new


def z_join(blocks, clamped):
    nodes = DEG * blocks + 1
    gather = np.zeros((nodes, blocks * N1))
    for element in range(blocks):
        for k in range(N1):
            gather[DEG * element + k, element * N1 + k] = 1.0
    if clamped:
        gather[0] = 0.0
        gather[nodes - 1] = 0.0
    return gather.T @ gather


def local(right_side, guess, material, lame, upper, lower_ratio):
    elems_x, elems_y, elems_z = material.shape
    cols = elems_x * elems_y
    lanes = N1 * elems_z
    nodes_z = DEG * elems_z - 1
    weights_np, derivative_np, ratio_np = gll_tables(DEG)
    eye_z = np.eye(elems_z)
    grad_np = np.kron(eye_z, derivative_np.T)
    join_np = z_join(elems_z, True)
    back_np = np.kron(eye_z, derivative_np) @ join_np
    grad_high, grad_low = np_halves(grad_np)
    back_high, back_low = np_halves(back_np)
    none = np.zeros_like(grad_high)
    joined = join_np.astype(jnp.bfloat16)
    grad_in = jnp.asarray(np.block([[grad_high, grad_low], [grad_high, none]]))
    back_in = jnp.asarray(
        np.block([[joined, none], [joined, none], [back_high, back_low], [back_high, none]])
    )
    all_join = z_join(elems_z, False).astype(jnp.bfloat16)
    join_in = jnp.asarray(np.concatenate([all_join, all_join], axis=0))

    weights_z = np.tile(weights_np, elems_z)
    ratio_z = np.tile(ratio_np, elems_z)
    weight_np = weights_np[:, None, None] * weights_np[None, :, None] * weights_z
    shape_w = (N1, N1, lanes)
    own_x = np.broadcast_to(ratio_np[:, None, None], shape_w)
    own_y = np.broadcast_to(ratio_np[None, :, None], shape_w)
    own_z = np.broadcast_to(ratio_z, shape_w)
    own_np = np.stack([own_x, own_y, own_z])
    weight_in = jnp.asarray(weight_np[:, :, None], jnp.float32)
    own_in = jnp.asarray(own_np[:, :, :, None], jnp.float32)
    sum_in = jnp.asarray((own_x + own_y + own_z)[:, :, None], jnp.float32)

    lam_el, mu_el = lame_fields(material, lame)
    lam_in = jnp.repeat(lam_el.reshape(cols, elems_z), N1, axis=1)
    mu_in = jnp.repeat(mu_el.reshape(cols, elems_z), N1, axis=1)

    upper_edge = upper[0]
    lower_edge = lower_ratio[0] * upper_edge
    center = (upper_edge + lower_edge) / 2.0
    radius = (upper_edge - lower_edge) / 2.0
    sigma_ratio = center / radius
    alphas = []
    betas = []
    for sweep_index in range(SWEEPS):
        alphas.append(jnp.float32(0.0))
        betas.append(1.0 / center)
        factor = 1.0 / sigma_ratio
        for step_index in range(CHEB - 1):
            factor_next = 1.0 / (2.0 * sigma_ratio - factor)
            alphas.append(factor_next * factor)
            betas.append(2.0 * factor_next / radius)
            factor = factor_next
    coef = jnp.stack([jnp.stack(alphas), jnp.stack(betas)])

    gather_z = jnp.asarray(clamped_gather(elems_z), dtype=jnp.float32)
    owned = clamped_gather(elems_z)
    owned[:, DEG::N1] = 0.0
    select_z = jnp.asarray(owned.T, dtype=jnp.float32)

    def enter(flat):
        split = flat.reshape(3, elems_x, DEG, elems_y, DEG, nodes_z)
        wide = jnp.matmul(split, gather_z, precision=highest)
        wide = wide.transpose(0, 2, 4, 1, 3, 5).reshape(3, DEG, DEG, cols, lanes)
        return jnp.pad(wide, ((0, 0), (0, 1), (0, 1), (0, 0), (0, 0)))

    def leave(wide):
        split = wide[:, :DEG, :DEG].reshape(3, DEG, DEG, elems_x, elems_y, lanes)
        split = split.transpose(0, 3, 1, 4, 2, 5)
        thin = jnp.matmul(split, select_z, precision=highest)
        return thin.reshape(3, DEG * elems_x, DEG * elems_y * nodes_z)

    whole = (3, N1, N1, cols, lanes)
    shape = jax.ShapeDtypeStruct(whole, jnp.float32)
    vmem = pl.BlockSpec(memory_space=pltpu.VMEM)
    big = pltpu.VMEM(whole, jnp.float32)
    small = pltpu.VMEM((N1, N1, cols, lanes), jnp.float32)
    face_x = pltpu.VMEM((SLOTS, 2, 3, N1, elems_y, lanes), jnp.float32)
    face_y = pltpu.VMEM((SLOTS, 2, 3, N1, elems_x, lanes), jnp.float32)
    corner = pltpu.VMEM((SLOTS, 4, 3, 1, lanes), jnp.float32)

    def kernel(*refs):
        smoother_kernel(SWEEPS * CHEB, elems_x, elems_y, derivative_np, *refs)

    field, resid = pl.pallas_call(
        kernel,
        out_shape=(shape, shape),
        in_specs=[pl.BlockSpec(memory_space=pltpu.SMEM)] + [vmem] * 10,
        out_specs=(vmem, vmem),
        scratch_shapes=[
            small,
            small,
            big,
            big,
            big,
            big,
            big,
            face_x,
            face_y,
            corner,
            face_x,
            face_y,
            corner,
            pltpu.SemaphoreType.DMA((SLOTS, 8)),
            pltpu.SemaphoreType.DMA((SLOTS, 8)),
        ],
        compiler_params=pltpu.CompilerParams(collective_id=0, has_side_effects=True),
    )(
        coef,
        enter(guess),
        enter(right_side),
        lam_in,
        mu_in,
        weight_in,
        own_in,
        sum_in,
        grad_in,
        back_in,
        join_in,
    )
    return (leave(field), leave(resid))


def solution(mesh):
    placed = (P(None, "gx", "gy"), P(None, "gx", "gy"), P("gx", "gy", None), P(), P(), P())
    return jax.shard_map(
        local,
        mesh=mesh,
        in_specs=placed,
        out_specs=(P(None, "gx", "gy"), P(None, "gx", "gy")),
        check_vma=False,
    )
```

time: 322 us -> 149 us (0.46); the launches traced: 316 us -> 149 us
  Pallas kernels: 0 us -> 121 us
  matrix products: 90.8 us -> 7.69 us
  waiting for transfers between devices: 67.3 us -> 0 us
  local copies, waits for them, and re-layouts: 80.8 us -> 17.2 us
  other arithmetic: 39.8 us -> 0.55 us
  starting transfers between devices: 32.7 us -> 0 us
    pallas_call x0 -> x1, Pallas kernels: none -> 121 us  [local(): pl.pallas_call(kernel, out_shape=(shape, shape), in_specs=[pl.BlockSpec(m...]
    dot_general x57 -> x4, matrix products: 90.7 us -> 6.84 us  [the longest x2 4.3 us: leave(): thin = jnp.matmul(split, select_z, precision=highest)]
    ppermute x30 -> x0, waiting for transfers between devices: 67.3 us -> none  [from_behind(): lax.ppermute(value, axis, [(i, (i + by) % size) for i in range(size)])]
    ppermute x30 -> x0, starting transfers between devices: 32.7 us -> none  [from_behind(): lax.ppermute(value, axis, [(i, (i + by) % size) for i in range(size)])]
    slice x62 -> x2, local copies, waits for them, and re-layouts: 27.1 us -> 1.46 us  [leave(): split = wide[:, :DEG, :DEG].reshape(3, DEG, DEG, elems_x, elems_y, lanes)]
    add x40 -> x0, other arithmetic: 22.5 us -> none  [the longest x7 8.4 us: element_forces(): mu_w * (gradients + jnp.swapaxes(gradients, 0, 1))]
    scatter-add x8 -> x0, local copies, waits for them, and re-layouts: 15.2 us -> none  [return_sums(): part_y = partial_value[:, :, :width_y].at[:, :, :1].add(from_y)]
    dot_general x7 -> x0, local copies, waits for them, and re-layouts: 7.69 us -> none  [element_forces(): jnp.einsum('pj,cxiyjz->cxiypz', derivative, element_vals, precision=highest)]
  transfers between devices with their start and end apart: 30 -> 0, of which waited for: 26 -> 0; matrix products, arithmetic and copies ran while one was open for 17% -> 0% of each run, Pallas kernels for 0% -> 0%
where the time goes in v1:
time: 149 us
  Pallas kernels  121 us (81%)
  local copies, waits for them, and re-layouts  17.2 us (12%)
  matrix products  7.69 us (5%)
  between operations  2.37 us (2%)
    pallas_call x1, Pallas kernels, local(): pl.pallas_call(kernel, out_shape=(shape, shape), in_specs=[pl.BlockSpec(m...  121 us
    reshape x2, local copies, waits for them, and re-layouts, enter(): split = flat.reshape(3, elems_x, DEG, elems_y, DEG, nodes_z)  5.89 us
    reshape x2, local copies, waits for them, and re-layouts, leave(): return thin.reshape(3, DEG * elems_x, DEG * elems_y * nodes_z)  4.51 us
    dot_general x2, matrix products, leave(): thin = jnp.matmul(split, select_z, precision=highest)  4.3 us

profile of v1, /device:TPU:0, one launch (start us, length us, event | category | flops | bytes accessed | tf_op | source)
XLA Modules:
  0.0 148.6 jit_solution(7167290963300679040)
XLA Ops:
  0.6 0.0 copy-start
  2.2 0.1 stack.42
  2.3 0.1 stack.37
  2.4 0.6 pad_maximum_fusion.refs_0_
  3.0 0.0 copy-done
  3.0 0.9 convolution_bitcast_fusion.2
  3.8 0.1 copy.23
  3.9 0.1 copy.22
  4.0 0.7 copy.24.refs_3_
  4.7 0.0 copy-start.4
  4.7 0.7 copy.25.refs_4_
  5.3 3.6 %reshape.37 = f32[3,4,7,4,7,111]{5,4,3,2,1,0:T(8,128)S(1)} reshape(f32[3,28,3108]{2,1,0:T(8,128)} %param.14) | data formatting | bytes 2088576 | tf_op jit(solution)/shard_map/reshape | solution.py:443
  8.9 0.0 copy-done.4
  8.9 1.3 convolution_bitcast_fusion
  10.2 0.3 copy.21
  10.5 0.0 copy-start.1
  10.6 1.3 pad.8.refs_2_
  11.9 0.4 copy-done.1
  12.3 2.3 %reshape.35 = f32[3,4,7,4,7,111]{5,4,3,2,1,0:T(8,128)S(1)} reshape(f32[3,28,3108]{2,1,0:T(8,128)S(1)} %copy-done.1) | data formatting | bytes 2088576 | tf_op jit(solution)/shard_map/reshape | solution.py:443
  14.6 1.3 convolution_bitcast_fusion.1
  15.8 0.3 copy.20
  16.2 1.3 pad.7.refs_1_
  17.5 120.8 %shard_map.149 = (f32[3,8,8,16,128]{4,3,2,1,0:T(8,128)}, f32[3,8,8,16,128]{4,3,2,1,0:T(8,128)}) custom-call(f32[2,6]{1,0:T(2,128)} %pad_maximum_fusion.refs_0_, f32[3,8,8,16,128]{4,3,2,1,0:T(8,128)} %pad.7.refs_1_, f32[3,8,8,16,128]{4,3,2,1,0:T(8,128)} %pad.8.refs_2_, f32[16,128]{1,0:T(8,128)} %copy.24.refs_3_, f32[16,128]{1,0:T(8,128)} %copy.25.refs_4_, ...), custom_call_target="tpu_custom_call" | custom-call | tf_op jit(solution)/shard_map/pallas_call | solution.py:466
  138.2 0.0 copy-start.3
  138.3 1.4 slice.14
  139.6 0.0 copy-done.3
  139.7 2.2 %fusion.2 = f32[3,4,7,4,7,111]{5,4,3,2,1,0:T(8,128)S(1)} fusion(f32[128,111,1,1,1,1]{0,1,5,4,3,2:T(8,128)S(1)} %copy-done.3, f32[3,7,7,4,4,128]{5,4,3,2,1,0:T(4,128)S(1)} %bitcast.53), kind=kOutput, calls=%fused_computation.4 | convolution fusion | flops 401006592 | bytes 2305344 | tf_op jit(solution)/shard_map/dot_general | solution.py:451
  141.8 0.0 copy-start.2
  141.8 2.3 %reshape.42 = f32[3,28,3108]{2,1,0:T(8,128)} reshape(f32[3,4,7,4,7,111]{5,4,3,2,1,0:T(8,128)S(1)} %fusion.2) | data formatting | bytes 2088576 | tf_op jit(solution)/shard_map/reshape | solution.py:452
  144.1 0.0 copy-done.2
  144.1 0.1 slice.15
  144.2 2.2 %fusion = f32[3,4,7,4,7,111]{5,4,3,2,1,0:T(8,128)S(1)} fusion(f32[128,111,1,1,1,1]{0,1,5,4,3,2:T(8,128)S(1)} %copy-done.3, f32[3,7,7,4,4,128]{5,4,3,2,1,0:T(4,128)S(1)} %bitcast.52), kind=kOutput, calls=%fused_computation.2 | convolution fusion | flops 401006592 | bytes 2305344 | tf_op jit(solution)/shard_map/dot_general | solution.py:451
  146.3 2.2 %reshape.44 = f32[3,28,3108]{2,1,0:T(8,128)} reshape(f32[3,4,7,4,7,111]{5,4,3,2,1,0:T(8,128)S(1)} %fusion) | data formatting | bytes 2088576 | tf_op jit(solution)/shard_map/reshape | solution.py:452
  (3 shorter events, 0.0 us)
Async XLA Ops:
  0.6 2.3 %copy-start = (f32[2,8]{1,0:T(2,128)S(1)}, f32[2,8]{1,0:T(2,128)}, u32[]{:S(2)}) copy-start(f32[2,8]{1,0:T(2,128)} %param.17) | copy-start | bytes 196
  4.7 4.3 %copy-start.4 = (f32[111,128,1,1,1,1]{1,0,5,4,3,2:T(8,128)S(1)}, f32[111,128,1,1,1,1]{1,0,5,4,3,2:T(8,128)}, u32[]{:S(2)}) copy-start(f32[111,128,1,1,1,1]{1,0,5,4,3,2:T(8,128)} %constant.43) | copy-start | bytes 170500
  10.5 1.7 %copy-start.1 = (f32[3,28,3108]{2,1,0:T(8,128)S(1)}, f32[3,28,3108]{2,1,0:T(8,128)}, u32[]{:S(2)}) copy-start(f32[3,28,3108]{2,1,0:T(8,128)} %param.15) | copy-start | bytes 3132868
  138.2 1.4 copy-start.3
  141.8 2.3 %copy-start.2 = (f32[3,8,8,16,128]{4,3,2,1,0:T(8,128)S(1)}, f32[3,8,8,16,128]{4,3,2,1,0:T(8,128)}, u32[]{:S(2)}) copy-start(f32[3,8,8,16,128]{4,3,2,1,0:T(8,128)} %get-tuple-element.5) | copy-start | bytes 4718596

commit v2 on v1

v2 whole, which is shorter than its diff:
```python
import jax
import jax.numpy as jnp
import numpy as np
from jax import lax
from jax.experimental import pallas as pl
from jax.experimental.pallas import tpu as pltpu
from jax.sharding import PartitionSpec as P

DEG = 7
SWEEPS = 2
CHEB = 3


highest = lax.Precision.HIGHEST


def legendre_pair(points, degree):
    prev_poly = points * 0.0 + 1.0
    this_poly = points * 1.0
    for order in range(2, degree + 1):
        next_poly = ((2 * order - 1) * points * this_poly - (order - 1) * prev_poly) / order
        prev_poly = this_poly
        this_poly = next_poly
    return (this_poly, prev_poly)


def gll_tables(degree):
    count = degree + 1
    points = -np.cos(np.pi * np.arange(count) / degree)
    for newton_step in range(60):
        this_poly, prev_poly = legendre_pair(points, degree)
        points = points - (points * this_poly - prev_poly) / (count * this_poly)
    values, unused_poly = legendre_pair(points, degree)
    weights = 2.0 / (degree * (degree + 1) * values**2)
    identity_np = np.eye(count)
    spacing = points[:, None] - points[None, :] + identity_np
    derivative = values[:, None] / (values[None, :] * spacing) * (1.0 - identity_np)
    derivative[0, 0] = -degree * (degree + 1) / 4.0
    derivative[degree, degree] = degree * (degree + 1) / 4.0
    stiff_ratio = (weights[:, None] * derivative**2).sum(0) / weights
    return (weights, derivative, stiff_ratio)


def clamped_gather(blocks):
    free_nodes = DEG * blocks - 1
    selector = np.zeros((free_nodes, blocks * (DEG + 1)), np.float32)
    for element in range(blocks):
        for node_idx in range(DEG + 1):
            target = DEG * element + node_idx - 1
            if 0 <= target < free_nodes:
                selector[target, element * (DEG + 1) + node_idx] = 1.0
    return selector


N1 = DEG + 1
SLOTS = 4


def halves(value):
    high = value.astype(jnp.bfloat16)
    low = (value - high.astype(jnp.float32)).astype(jnp.bfloat16)
    return high, low


def np_halves(matrix):
    high = np.asarray(matrix, np.float32).astype(jnp.bfloat16)
    low = (np.asarray(matrix, np.float64) - high.astype(np.float64)).astype(jnp.bfloat16)
    return high, low


def apply_pairs(matrix, values):
    half = N1 // 2
    even = [values[i] + values[DEG - i] for i in range(half)]
    odd = [values[i] - values[DEG - i] for i in range(half)]
    outs = [None] * N1
    for p in range(half):
        plus = None
        minus = None
        for i in range(half):
            by_even = float(np.float32((matrix[p, i] + matrix[p, DEG - i]) / 2))
            by_odd = float(np.float32((matrix[p, i] - matrix[p, DEG - i]) / 2))
            plus = by_even * even[i] if plus is None else plus + by_even * even[i]
            minus = by_odd * odd[i] if minus is None else minus + by_odd * odd[i]
        outs[p] = minus + plus
        outs[DEG - p] = minus - plus
    return outs


def smoother_kernel(
    steps,
    elems_x,
    elems_y,
    derivative,
    lame,
    upper,
    lower_ratio,
    guess_in,
    source_in,
    material,
    weight_in,
    own_in,
    sum_in,
    spread_in,
    gather_in,
    select_in,
    grad_in,
    back_in,
    join_in,
    smoothed_out,
    residual_out,
    coef,
    field,
    resid,
    source,
    lam_w,
    mu_w,
    inverse,
    change,
    grad_x,
    grad_y,
    grad_z,
    flat_a,
    flat_b,
    send_x,
    send_y,
    send_c,
    recv_x,
    recv_y,
    recv_c,
    send_sem,
    recv_sem,
):
    cols = elems_x * elems_y
    size_x = lax.axis_size("gx")
    size_y = lax.axis_size("gy")
    me_x = lax.axis_index("gx")
    me_y = lax.axis_index("gy")
    near_x = (lax.rem(me_x + size_x - 1, size_x), lax.rem(me_x + 1, size_x))
    near_y = (lax.rem(me_y + size_y - 1, size_y), lax.rem(me_y + 1, size_y))
    partners = [(near_x[0], me_y), (near_x[1], me_y), (me_x, near_y[0]), (me_x, near_y[1])]
    partners += [(near_x[a], near_y[b]) for a in range(2) for b in range(2)]

    barrier = pltpu.get_barrier_semaphore()
    for partner in partners:
        pl.semaphore_signal(
            barrier, inc=1, device_id=partner, device_id_type=pl.DeviceIdType.MESH
        )
    pl.semaphore_wait(barrier, len(partners))

    def copies(slot, c):
        made = []
        for d in range(8):
            if d < 2:
                src, dst = send_x.at[slot, c, d], recv_x.at[slot, c, 1 - d]
            elif d < 4:
                src, dst = send_y.at[slot, c, d - 2], recv_y.at[slot, c, 3 - d]
            else:
                src, dst = send_c.at[slot, c, d - 4], recv_c.at[slot, c, 7 - d]
            mirror = (1, 0, 3, 2, 7, 6, 5, 4)[d]
            made.append(
                pltpu.make_async_remote_copy(
                    src_ref=src,
                    dst_ref=dst,
                    send_sem=send_sem.at[slot, c, d],
                    recv_sem=recv_sem.at[slot, c, mirror],
                    device_id=partners[d],
                    device_id_type=pl.DeviceIdType.MESH,
                )
            )
        return made

    rows = lax.broadcasted_iota(jnp.int32, (N1 * cols, 128), 0) % cols
    row_x = rows % elems_x
    inner_low_y = rows >= elems_x
    inner_high_y = rows < cols - elems_x
    inner_low_x = row_x >= 1
    inner_high_x = row_x < elems_x - 1
    last_x = elems_x - 1
    last_y = cols - elems_x
    flat = (N1 * cols, 128)
    full = (N1, cols, 128)

    def local_sum(ref, c):
        zero = jnp.zeros(flat, jnp.float32)
        low = ref[c, 0].reshape(flat)
        high = ref[c, DEG].reshape(flat)
        to_low = jnp.where(inner_low_x, pltpu.roll(high, 1, 0), zero)
        to_high = jnp.where(inner_high_x, pltpu.roll(low, N1 * cols - 1, 0), zero)
        ref[c, 0] = (low + to_low).reshape(full)
        ref[c, DEG] = (high + to_high).reshape(full)
        low = ref[c, :, 0].reshape(flat)
        high = ref[c, :, DEG].reshape(flat)
        to_low = jnp.where(inner_low_y, pltpu.roll(high, elems_x, 0), zero)
        to_high = jnp.where(inner_high_y, pltpu.roll(low, N1 * cols - elems_x, 0), zero)
        ref[c, :, 0] = (low + to_low).reshape(full)
        ref[c, :, DEG] = (high + to_high).reshape(full)

    def post(ref, slot, c):
        send_y[slot, c, 0] = ref[c, :, 0, 0:elems_x, :]
        send_y[slot, c, 1] = ref[c, :, DEG, last_y:cols, :]
        for b in range(elems_y):
            at = b * elems_x
            send_x[slot, c, 0, :, b : b + 1, :] = ref[c, 0, :, at : at + 1, :]
            at = b * elems_x + last_x
            send_x[slot, c, 1, :, b : b + 1, :] = ref[c, DEG, :, at : at + 1, :]
        for a in range(2):
            for b in range(2):
                at = a * last_x + b * last_y
                send_c[slot, c, 2 * a + b] = ref[c, a * DEG, b * DEG, at : at + 1, :]
        for copy in copies(slot, c):
            copy.start()

    def collect(ref, slot, c):
        for copy in copies(slot, c):
            copy.wait()
        ref[c, :, 0, 0:elems_x, :] += recv_y[slot, c, 0]
        ref[c, :, DEG, last_y:cols, :] += recv_y[slot, c, 1]
        for b in range(elems_y):
            at = b * elems_x
            ref[c, 0, :, at : at + 1, :] += recv_x[slot, c, 0, :, b : b + 1, :]
            at = b * elems_x + last_x
            ref[c, DEG, :, at : at + 1, :] += recv_x[slot, c, 1, :, b : b + 1, :]
        for a in range(2):
            for b in range(2):
                at = a * last_x + b * last_y
                ref[c, a * DEG, b * DEG, at : at + 1, :] += recv_c[slot, c, 2 * a + b]

    nodes_x = DEG * elems_x
    nodes_y = DEG * elems_y
    nodes_z = guess_in.shape[2] // nodes_y
    pad_x = flat_a.shape[1]
    zeros_big = jnp.zeros((N1, cols, 128), jnp.float32)

    @pl.loop(0, nodes_y)
    def _(y):
        flat_a[y] = jnp.zeros((pad_x, 128), jnp.float32)
        flat_b[y] = jnp.zeros((pad_x, 128), jnp.float32)

    def through(src, dst, matrix):
        @pl.loop(0, elems_y)
        def _(b):
            pick = pl.ds(b * DEG, DEG)
            parts = halves(src[pick].reshape(DEG * pad_x, 128))
            dst[pick] = jnp.dot(
                jnp.concatenate(parts, axis=1), matrix[...], preferred_element_type=jnp.float32
            ).reshape(DEG, pad_x, 128)

    def enter(flat_in, ref, c):
        lines = flat_in[c]
        for y in range(nodes_y):
            flat_a[y, 0:nodes_x, 0:nodes_z] = lines[:, y * nodes_z : (y + 1) * nodes_z]
        through(flat_a, flat_b, gather_in)
        ref[c, DEG] = zeros_big
        ref[c, :, DEG] = zeros_big
        for b in range(elems_y):
            for j in range(DEG):
                for i in range(DEG):
                    ref[c, i, j, b * elems_x : (b + 1) * elems_x, :] = flat_b[
                        b * DEG + j, pl.ds(i, elems_x, stride=DEG), :
                    ]

    def leave(ref, flat_out, c):
        for b in range(elems_y):
            for j in range(DEG):
                for i in range(DEG):
                    flat_b[b * DEG + j, pl.ds(i, elems_x, stride=DEG), :] = ref[
                        c, i, j, b * elems_x : (b + 1) * elems_x, :
                    ]
        through(flat_b, flat_a, select_in)
        lines = [flat_a[y, 0:nodes_x, 0:nodes_z] for y in range(nodes_y)]
        flat_out[c] = jnp.concatenate(lines, axis=1)

    @pl.loop(0, 3)
    def _(c):
        enter(guess_in, field, c)
        local_sum(field, c)
        post(field, 0, c)

    upper_edge = jnp.full((1, 128), upper[0], jnp.float32)
    lower_edge = lower_ratio[0] * upper_edge
    center = (upper_edge + lower_edge) / 2.0
    radius = (upper_edge - lower_edge) / 2.0
    sigma_ratio = center / radius
    for sweep in range(SWEEPS):
        coef[0, sweep * CHEB] = jnp.zeros((1, 128), jnp.float32)
        coef[1, sweep * CHEB] = 1.0 / center
        factor = 1.0 / sigma_ratio
        for later in range(1, CHEB):
            factor_next = 1.0 / (2.0 * sigma_ratio - factor)
            coef[0, sweep * CHEB + later] = factor_next * factor
            coef[1, sweep * CHEB + later] = 2.0 * factor_next / radius
            factor = factor_next

    kinds = jnp.concatenate([material[:, b, :] for b in range(elems_y)], axis=0)
    tables = []
    for row in range(2):
        picked = jnp.zeros(kinds.shape, jnp.float32)
        for kind in range(lame.shape[1]):
            picked = jnp.where(kinds == kind, lame[row, kind], picked)
        tables.append(
            jnp.dot(picked, spread_in[...], precision=highest, preferred_element_type=jnp.float32)
        )
    lam_all, mu_all = tables

    @pl.loop(0, N1)
    def _(i):
        for j in range(N1):
            lam_w[i, j] = lam_all * weight_in[i, j]
            mu_w[i, j] = mu_all * weight_in[i, j]

    @pl.loop(0, 3 * N1)
    def _(at):
        c = at // N1
        i = at % N1
        pieces = []
        for j in range(N1):
            own = own_in[c, i, j]
            pieces.append(lam_w[i, j] * own + mu_w[i, j] * (sum_in[i, j] + own))
        high, low = halves(jnp.concatenate(pieces, axis=0))
        summed = jnp.dot(
            jnp.concatenate([high, low], axis=1), join_in[...], preferred_element_type=jnp.float32
        )
        inverse[c, i] = summed.reshape(N1, cols, 128)

    for c in range(3):
        local_sum(inverse, c)
        post(inverse, 1, c)

    def gradients(c):
        @pl.loop(0, N1)
        def _(i):
            high, low = halves(field[c, i].reshape(flat))
            both = jnp.dot(
                jnp.concatenate([high, low], axis=1),
                grad_in[...],
                preferred_element_type=jnp.float32,
            )
            for p, out in enumerate(apply_pairs(derivative, [field[c, k, i] for k in range(N1)])):
                grad_x[c, p, i] = out
            for q, out in enumerate(apply_pairs(derivative, [field[c, i, k] for k in range(N1)])):
                grad_y[c, i, q] = out
            grad_z[c, i] = (both[:, :128] + both[:, 128:]).reshape(full)

    def stresses():
        @pl.loop(0, N1)
        def _(i):
            for j in range(N1):
                lam = lam_w[i, j]
                mu = mu_w[i, j]
                d00, d11, d22 = grad_x[0, i, j], grad_y[1, i, j], grad_z[2, i, j]
                base = lam * (d00 + d11 + d22)
                two = mu + mu
                grad_x[0, i, j] = two * d00 + base
                grad_y[1, i, j] = two * d11 + base
                grad_z[2, i, j] = two * d22 + base
                s01 = mu * (grad_x[1, i, j] + grad_y[0, i, j])
                s02 = mu * (grad_x[2, i, j] + grad_z[0, i, j])
                s12 = mu * (grad_y[2, i, j] + grad_z[1, i, j])
                grad_x[1, i, j] = s01
                grad_y[0, i, j] = s01
                grad_x[2, i, j] = s02
                grad_z[0, i, j] = s02
                grad_y[2, i, j] = s12
                grad_z[1, i, j] = s12

    def forces(c):
        @pl.loop(0, N1)
        def _(j):
            for p, out in enumerate(apply_pairs(derivative.T, [grad_x[c, k, j] for k in range(N1)])):
                resid[c, p, j] = out

        @pl.loop(0, N1)
        def _(i):
            outs = apply_pairs(derivative.T, [grad_y[c, i, k] for k in range(N1)])
            inner = jnp.concatenate([resid[c, i, q] + outs[q] for q in range(N1)], axis=0)
            parts = halves(grad_z[c, i].reshape(flat)) + halves(inner)
            both = jnp.dot(
                jnp.concatenate(parts, axis=1), back_in[...], preferred_element_type=jnp.float32
            )
            resid[c, i] = source[c, i] - (both[:, :128] + both[:, 128:]).reshape(full)

    def residuals(slot):
        stresses()

        @pl.loop(0, 3)
        def _(c):
            forces(c)
            local_sum(resid, c)
            post(resid, slot, c)

    @pl.loop(0, 3)
    def _(c):
        enter(source_in, source, c)

    @pl.loop(0, 3)
    def _(c):
        collect(field, 0, c)
        gradients(c)

    @pl.loop(0, 3)
    def _(c):
        collect(inverse, 1, c)

        @pl.loop(0, N1)
        def _(i):
            inverse[c, i] = 1.0 / inverse[c, i]
            change[c, i] = zeros_big

    @pl.loop(0, steps)
    def _(step):
        slot = 2 + step % 2
        residuals(slot)

        @pl.loop(0, 3)
        def _(c):
            collect(resid, slot, c)
            alpha = coef[0, step]
            beta = coef[1, step]

            @pl.loop(0, N1)
            def _(i):
                new = alpha * change[c, i] + beta * (inverse[c, i] * resid[c, i])
                change[c, i] = new
                field[c, i] += new

            gradients(c)

    slot = 2 + steps % 2
    residuals(slot)

    @pl.loop(0, 3)
    def _(c):
        leave(field, smoothed_out, c)

    @pl.loop(0, 3)
    def _(c):
        collect(resid, slot, c)
        leave(resid, residual_out, c)


def z_join(blocks, clamped):
    nodes = DEG * blocks + 1
    gather = np.zeros((nodes, blocks * N1))
    for element in range(blocks):
        for k in range(N1):
            gather[DEG * element + k, element * N1 + k] = 1.0
    if clamped:
        gather[0] = 0.0
        gather[nodes - 1] = 0.0
    return gather.T @ gather


def local(right_side, guess, material, lame, upper, lower_ratio):
    elems_x, elems_y, elems_z = material.shape
    cols = elems_x * elems_y
    lanes = N1 * elems_z
    nodes_z = DEG * elems_z - 1
    weights_np, derivative_np, ratio_np = gll_tables(DEG)
    eye_z = np.eye(elems_z)
    grad_np = np.kron(eye_z, derivative_np.T)
    join_np = z_join(elems_z, True)
    back_np = np.kron(eye_z, derivative_np) @ join_np
    grad_high, grad_low = np_halves(grad_np)
    back_high, back_low = np_halves(back_np)
    none = np.zeros_like(grad_high)
    joined = join_np.astype(jnp.bfloat16)
    grad_in = jnp.asarray(np.block([[grad_high, grad_low], [grad_high, none]]))
    back_in = jnp.asarray(
        np.block([[back_high, back_low], [back_high, none], [joined, none], [joined, none]])
    )
    all_join = z_join(elems_z, False).astype(jnp.bfloat16)
    join_in = jnp.asarray(np.concatenate([all_join, all_join], axis=0))

    weights_z = np.tile(weights_np, elems_z)
    ratio_z = np.tile(ratio_np, elems_z)
    weight_np = weights_np[:, None, None] * weights_np[None, :, None] * weights_z
    shape_w = (N1, N1, lanes)
    own_x = np.broadcast_to(ratio_np[:, None, None], shape_w)
    own_y = np.broadcast_to(ratio_np[None, :, None], shape_w)
    own_z = np.broadcast_to(ratio_z, shape_w)
    own_np = np.stack([own_x, own_y, own_z])
    weight_in = jnp.asarray(weight_np[:, :, None], jnp.float32)
    own_in = jnp.asarray(own_np[:, :, :, None], jnp.float32)
    sum_in = jnp.asarray((own_x + own_y + own_z)[:, :, None], jnp.float32)

    gather_np = clamped_gather(elems_z)
    nodes_z = gather_np.shape[0]
    owned_np = gather_np.copy()
    owned_np[:, DEG::N1] = 0.0
    enter_np = np.zeros((lanes, lanes))
    enter_np[:nodes_z] = gather_np
    leave_np = np.zeros((lanes, lanes))
    leave_np[:, :nodes_z] = owned_np.T
    gather_in = jnp.asarray(np.concatenate([enter_np, enter_np], axis=0).astype(jnp.bfloat16))
    select_in = jnp.asarray(np.concatenate([leave_np, leave_np], axis=0).astype(jnp.bfloat16))
    spread_in = jnp.asarray(np.kron(eye_z, np.ones((1, N1))), dtype=jnp.float32)

    pad_x = -(-DEG * elems_x // 8) * 8
    whole = (3, N1, N1, cols, lanes)
    vmem = pl.BlockSpec(memory_space=pltpu.VMEM)
    smem = pl.BlockSpec(memory_space=pltpu.SMEM)
    big = pltpu.VMEM(whole, jnp.float32)
    small = pltpu.VMEM((N1, N1, cols, lanes), jnp.float32)
    lines = pltpu.VMEM((DEG * elems_y, pad_x, lanes), jnp.float32)
    face_x = pltpu.VMEM((SLOTS, 3, 2, N1, elems_y, lanes), jnp.float32)
    face_y = pltpu.VMEM((SLOTS, 3, 2, N1, elems_x, lanes), jnp.float32)
    corner = pltpu.VMEM((SLOTS, 3, 4, 1, lanes), jnp.float32)
    shape = jax.ShapeDtypeStruct(guess.shape, jnp.float32)

    def kernel(*refs):
        smoother_kernel(SWEEPS * CHEB, elems_x, elems_y, derivative_np, *refs)

    return pl.pallas_call(
        kernel,
        out_shape=(shape, shape),
        in_specs=[smem] * 3 + [vmem] * 12,
        out_specs=(vmem, vmem),
        scratch_shapes=[pltpu.VMEM((2, SWEEPS * CHEB, 1, lanes), jnp.float32)]
        + [big] * 3
        + [small] * 2
        + [big] * 5
        + [lines] * 2
        + [face_x, face_y, corner] * 2
        + [pltpu.SemaphoreType.DMA((SLOTS, 3, 8))] * 2,
        compiler_params=pltpu.CompilerParams(collective_id=0, has_side_effects=True),
    )(
        lame,
        upper,
        lower_ratio,
        guess,
        right_side,
        material,
        weight_in,
        own_in,
        sum_in,
        spread_in,
        gather_in,
        select_in,
        grad_in,
        back_in,
        join_in,
    )


def solution(mesh):
    placed = (P(None, "gx", "gy"), P(None, "gx", "gy"), P("gx", "gy", None), P(), P(), P())
    return jax.shard_map(
        local,
        mesh=mesh,
        in_specs=placed,
        out_specs=(P(None, "gx", "gy"), P(None, "gx", "gy")),
        check_vma=False,
    )
```

time: 149 us -> 118 us (0.79)
  local copies, waits for them, and re-layouts: 17.2 us -> 3.53 us
  Pallas kernels: 121 us -> 112 us
  matrix products: 7.69 us -> 0 us
    reshape x8 -> x0, local copies, waits for them, and re-layouts: 11.7 us -> none  [the longest x2 5.89 us: enter(): split = flat.reshape(3, elems_x, DEG, elems_y, DEG, nodes_z)]
    pallas_call x1, Pallas kernels: 121 us -> 112 us  [local(): pl.pallas_call(kernel, out_shape=(shape, shape), in_specs=[smem] * 3 + [v...]
    dot_general x5 -> x0, matrix products: 7.69 us -> none  [the longest x2 4.3 us: leave(): thin = jnp.matmul(split, select_z, precision=highest)]
    unnamed x10 -> x4, local copies, waits for them, and re-layouts: 0.4 us -> 3.53 us
    pad x2 -> x0, local copies, waits for them, and re-layouts: 2.66 us -> none  [enter(): return jnp.pad(wide, ((0, 0), (0, 1), (0, 1), (0, 0), (0, 0)))]
where the time goes in v2:
time: 118 us
  Pallas kernels  112 us (95%)
  local copies, waits for them, and re-layouts  3.53 us (3%)
  between operations  1.94 us (2%)
    pallas_call x1, Pallas kernels, local(): pl.pallas_call(kernel, out_shape=(shape, shape), in_specs=[smem] * 3 + [v...  112 us
    unnamed x4, local copies, waits for them, and re-layouts  3.53 us

profile of v2, /device:TPU:0, one launch (start us, length us, event | category | flops | bytes accessed | tf_op | source)
XLA Modules:
  0.0 117.7 jit_solution(12375308129284776367)
XLA Ops:
  1.9 112.2 %shard_map.158 = (f32[3,28,3108]{2,1,0:T(8,128)}, f32[3,28,3108]{2,1,0:T(8,128)}) custom-call(f32[2,8]{1,0:T(2,128)} %refs_0_.1, f32[1]{0:T(128)S(6)} %copy.19.refs_1_, f32[1]{0:T(128)S(6)} %copy.20.refs_2_, f32[3,28,3108]{2,1,0:T(8,128)} %refs_3_.1, f32[3,28,3108]{2,1,0:T(8,128)} %refs_4_.1, s32[4,4,16]{2,1,0:T(4,128)} %refs_5_.1, ...), custom_call_target="tpu_custom_call" | custom-call | tf_op jit(solution)/shard_map/pallas_call | solution.py:513
  114.1 0.0 copy-start
  114.1 2.5 %copy.21 = f32[3,28,3108]{2,1,0:T(8,128)} copy(f32[3,28,3108]{2,1,0:T(8,128)} %get-tuple-element.4) | data formatting | bytes 2088576
  116.6 0.0 copy-done
  116.6 1.0 copy.22
Async XLA Ops:
  114.1 2.5 %copy-start = (f32[3,28,3108]{2,1,0:T(8,128)S(1)}, f32[3,28,3108]{2,1,0:T(8,128)}, u32[]{:S(2)}) copy-start(f32[3,28,3108]{2,1,0:T(8,128)} %get-tuple-element.5) | copy-start | bytes 3132868

commit v3 on v2

--- a/solution.py
+++ b/solution.py
@@ -237,7 +237,7 @@
         flat_b[y] = jnp.zeros((pad_x, 128), jnp.float32)
 
     def through(src, dst, matrix):
-        @pl.loop(0, elems_y)
+        @pl.loop(0, elems_y, unroll=elems_y)
         def _(b):
             pick = pl.ds(b * DEG, DEG)
             parts = halves(src[pick].reshape(DEG * pad_x, 128))
@@ -327,7 +327,7 @@
         post(inverse, 1, c)
 
     def gradients(c):
-        @pl.loop(0, N1)
+        @pl.loop(0, N1, unroll=N1)
         def _(i):
             high, low = halves(field[c, i].reshape(flat))
             both = jnp.dot(
@@ -342,7 +342,7 @@
             grad_z[c, i] = (both[:, :128] + both[:, 128:]).reshape(full)
 
     def stresses():
-        @pl.loop(0, N1)
+        @pl.loop(0, N1, unroll=2)
         def _(i):
             for j in range(N1):
                 lam = lam_w[i, j]
@@ -364,12 +364,12 @@
                 grad_z[1, i, j] = s12
 
     def forces(c):
-        @pl.loop(0, N1)
+        @pl.loop(0, N1, unroll=N1)
         def _(j):
             for p, out in enumerate(apply_pairs(derivative.T, [grad_x[c, k, j] for k in range(N1)])):
                 resid[c, p, j] = out
 
-        @pl.loop(0, N1)
+        @pl.loop(0, N1, unroll=N1)
         def _(i):
             outs = apply_pairs(derivative.T, [grad_y[c, i, k] for k in range(N1)])
             inner = jnp.concatenate([resid[c, i, q] + outs[q] for q in range(N1)], axis=0)
@@ -417,7 +417,7 @@
             alpha = coef[0, step]
             beta = coef[1, step]
 
-            @pl.loop(0, N1)
+            @pl.loop(0, N1, unroll=4)
             def _(i):
                 new = alpha * change[c, i] + beta * (inverse[c, i] * resid[c, i])
                 change[c, i] = new

time: 118 us -> 81.2 us (0.69)
  Pallas kernels: 112 us -> 75.5 us
    pallas_call x1, Pallas kernels: 112 us -> 75.5 us  [local(): pl.pallas_call(kernel, out_shape=(shape, shape), in_specs=[smem] * 3 + [v...]
where the time goes in v3:
time: 81.2 us; the launch traced here: 81 us
  Pallas kernels  75.5 us (93%)
  local copies, waits for them, and re-layouts  3.53 us (4%)
  between operations  1.94 us (2%)
    pallas_call x1, Pallas kernels, local(): pl.pallas_call(kernel, out_shape=(shape, shape), in_specs=[smem] * 3 + [v...  75.5 us
    unnamed x4, local copies, waits for them, and re-layouts  3.53 us

profile of v3, /device:TPU:0, one launch (start us, length us, event | category | flops | bytes accessed | tf_op | source)
XLA Modules:
  0.0 81.0 jit_solution(1983389273511769041)
XLA Ops:
  1.9 75.5 %shard_map.158 = (f32[3,28,3108]{2,1,0:T(8,128)}, f32[3,28,3108]{2,1,0:T(8,128)}) custom-call(f32[2,8]{1,0:T(2,128)} %refs_0_.1, f32[1]{0:T(128)S(6)} %copy.19.refs_1_, f32[1]{0:T(128)S(6)} %copy.20.refs_2_, f32[3,28,3108]{2,1,0:T(8,128)} %refs_3_.1, f32[3,28,3108]{2,1,0:T(8,128)} %refs_4_.1, s32[4,4,16]{2,1,0:T(4,128)} %refs_5_.1, ...), custom_call_target="tpu_custom_call" | custom-call | tf_op jit(solution)/shard_map/pallas_call | solution.py:513
  77.5 0.0 copy-start
  77.5 2.5 %copy.21 = f32[3,28,3108]{2,1,0:T(8,128)} copy(f32[3,28,3108]{2,1,0:T(8,128)} %get-tuple-element.4) | data formatting | bytes 2088576
  80.0 0.0 copy-done
  80.0 1.0 %copy.22 = f32[3,28,3108]{2,1,0:T(8,128)} copy(f32[3,28,3108]{2,1,0:T(8,128)S(1)} %copy-done) | data formatting | bytes 2088576
Async XLA Ops:
  77.5 2.5 %copy-start = (f32[3,28,3108]{2,1,0:T(8,128)S(1)}, f32[3,28,3108]{2,1,0:T(8,128)}, u32[]{:S(2)}) copy-start(f32[3,28,3108]{2,1,0:T(8,128)} %get-tuple-element.5) | copy-start | bytes 3132868

commit v4 on v3

--- a/solution.py
+++ b/solution.py
@@ -308,7 +308,7 @@
             lam_w[i, j] = lam_all * weight_in[i, j]
             mu_w[i, j] = mu_all * weight_in[i, j]
 
-    @pl.loop(0, 3 * N1)
+    @pl.loop(0, 3 * N1, unroll=N1)
     def _(at):
         c = at // N1
         i = at % N1
@@ -342,7 +342,7 @@
             grad_z[c, i] = (both[:, :128] + both[:, 128:]).reshape(full)
 
     def stresses():
-        @pl.loop(0, N1, unroll=2)
+        @pl.loop(0, N1, unroll=N1)
         def _(i):
             for j in range(N1):
                 lam = lam_w[i, j]
@@ -417,7 +417,7 @@
             alpha = coef[0, step]
             beta = coef[1, step]
 
-            @pl.loop(0, N1, unroll=4)
+            @pl.loop(0, N1, unroll=N1)
             def _(i):
                 new = alpha * change[c, i] + beta * (inverse[c, i] * resid[c, i])
                 change[c, i] = new

time: 81.2 us -> 78.1 us (0.962)
  Pallas kernels: 75.5 us -> 72.5 us
    pallas_call x1, Pallas kernels: 75.5 us -> 72.5 us  [local(): pl.pallas_call(kernel, out_shape=(shape, shape), in_specs=[smem] * 3 + [v...]
where the time goes in v4:
time: 78.1 us; the launch traced here: 78 us
  Pallas kernels  72.5 us (93%)
  local copies, waits for them, and re-layouts  3.53 us (5%)
  between operations  1.94 us (2%)
    pallas_call x1, Pallas kernels, local(): pl.pallas_call(kernel, out_shape=(shape, shape), in_specs=[smem] * 3 + [v...  72.5 us
    unnamed x4, local copies, waits for them, and re-layouts  3.53 us

profile of v4, /device:TPU:0, one launch (start us, length us, event | category | flops | bytes accessed | tf_op | source)
XLA Modules:
  0.0 78.0 jit_solution(13085812233169320994)
XLA Ops:
  1.9 72.5 %shard_map.158 = (f32[3,28,3108]{2,1,0:T(8,128)}, f32[3,28,3108]{2,1,0:T(8,128)}) custom-call(f32[2,8]{1,0:T(2,128)} %refs_0_.1, f32[1]{0:T(128)S(6)} %copy.19.refs_1_, f32[1]{0:T(128)S(6)} %copy.20.refs_2_, f32[3,28,3108]{2,1,0:T(8,128)} %refs_3_.1, f32[3,28,3108]{2,1,0:T(8,128)} %refs_4_.1, s32[4,4,16]{2,1,0:T(4,128)} %refs_5_.1, ...), custom_call_target="tpu_custom_call" | custom-call | tf_op jit(solution)/shard_map/pallas_call | solution.py:513
  74.4 0.0 copy-start
  74.4 2.5 %copy.21 = f32[3,28,3108]{2,1,0:T(8,128)} copy(f32[3,28,3108]{2,1,0:T(8,128)} %get-tuple-element.4) | data formatting | bytes 2088576
  76.9 0.0 copy-done
  76.9 1.0 %copy.22 = f32[3,28,3108]{2,1,0:T(8,128)} copy(f32[3,28,3108]{2,1,0:T(8,128)S(1)} %copy-done) | data formatting | bytes 2088576
Async XLA Ops:
  74.4 2.5 %copy-start = (f32[3,28,3108]{2,1,0:T(8,128)S(1)}, f32[3,28,3108]{2,1,0:T(8,128)}, u32[]{:S(2)}) copy-start(f32[3,28,3108]{2,1,0:T(8,128)} %get-tuple-element.5) | copy-start | bytes 3132868
